TPU v7x, 64 devices: a 2x2x8 block of a 4x4x8 slice. The times are simulated.
64 devices in a mesh: dp: 8 (over x, y, core), tp: 8 (over z).
Axes of the slice: x: 2, y: 2, z: 8, core: 2. Of those that a mesh axis runs over, the one named last changes fastest.
The devices are a block of a 4x4x8 slice.
Arguments:
- x: bfloat16 [16384, 2304], P('dp'), parts along dimension 0
- dy: bfloat16 [16384, 2304], P('dp'), parts along dimension 0
- gate: bfloat16 [16384, 9216], P('dp', 'tp'), parts along dimension 0
- up: bfloat16 [16384, 9216], P('dp', 'tp'), parts along dimension 0
- w_gate: bfloat16 [2304, 9216], P(None, 'tp')
- w_up: bfloat16 [2304, 9216], P(None, 'tp')
- w_down: bfloat16 [9216, 2304], P('tp')
Outputs:
- output 1: bfloat16 [16384, 2304], P('dp'), parts along dimension 0
- output 2: bfloat16 [18432, 9216], P('dp', 'tp'), parts along dimension 0
- output 3: bfloat16 [18432, 9216], P('dp', 'tp'), parts along dimension 0
- output 4: bfloat16 [73728, 2304], P(('dp', 'tp')), parts along dimension 0
There are 8 independent parts. A program takes and returns all parts, laid end to end along the dimension named above; an argument that names none is the same for every part.
All inputs are finite; a program needn't handle non-finite values.
Results may differ from a plain program's by a relative error of at most 0.012.
Values are sent between devices in bfloat16 or wider.
A program may use at most 768 MiB of HBM per device.

v0:
```python
import jax
import jax.numpy as jnp
from jax import lax
from jax.sharding import PartitionSpec as P


def act(gate, up):
    return jax.nn.gelu(gate) * up


def solution(mesh):
    def step(x, dy, gate, up, w_gate, w_up, w_down):
        hidden, back = jax.vjp(act, gate.astype(jnp.float32), up.astype(jnp.float32))
        d_hidden = jnp.dot(dy, w_down.T, preferred_element_type=jnp.float32)
        d_gate, d_up = (g.astype(jnp.bfloat16) for g in back(d_hidden))
        term = jnp.dot(d_gate, w_gate.T, preferred_element_type=jnp.float32) + jnp.dot(d_up, w_up.T, preferred_element_type=jnp.float32)
        dx = lax.psum(term.astype(jnp.bfloat16), "tp")
        dw_gate = jnp.dot(x.T, d_gate, preferred_element_type=jnp.float32)
        dw_up = jnp.dot(x.T, d_up, preferred_element_type=jnp.float32)
        dw_down = jnp.dot(hidden.astype(jnp.bfloat16).T, dy, preferred_element_type=jnp.float32)
        return dx, *(g.astype(jnp.bfloat16) for g in (dw_gate, dw_up, dw_down))

    tokens, columns, rows = P("dp", None), P(None, "tp"), P("tp", None)
    return jax.shard_map(
        step,
        mesh=mesh,
        in_specs=(tokens, tokens, P("dp", "tp"), P("dp", "tp"), columns, columns, rows),
        out_specs=(tokens, P("dp", "tp"), P("dp", "tp"), P(("dp", "tp"), None)),
        check_vma=False,
    )
```

profile of v0, /device:TPU:21, one launch (start us, length us, event | category | flops | bytes accessed | tf_op | source)
XLA Modules:
  0.0 293.7 jit_solution(14019624609875053343)
XLA Ops:
  7.2 0.1 all-reduce.2.cloned.1.call-start
  7.2 0.0 copy-start
  7.3 26.2 %fusion.6 = (bf16[2048,1152]{1,0:T(8,128)(2,1)}, f32[2048,1152]{1,0:T(8,128)}) fusion(bf16[2048,1152]{1,0:T(8,128)(2,1)} %param.9, bf16[2048,1152]{1,0:T(8,128)(2,1)} %param.10, bf16[2048,2304]{1,0:T(8,128)(2,1)} %param.8, bf16[1152,2304]{1,0:T(8,128)(2,1)} %param.13), kind=kOutput, calls=%fused_computation.17 | convolution fusion | flops 10925899776 | bytes 38338560 | tf_op jit(solution)/shard_map/dot_general | solution.py:14
  33.4 0.0 copy-done
  33.5 16.9 %fusion.21 = f32[2048,2304]{1,0:T(8,128)} fusion(bf16[2048,1152]{1,0:T(8,128)(2,1)} %get-tuple-element.8, bf16[2304,1152]{1,0:T(8,128)(2,1)S(1)} %copy-done), kind=kOutput, calls=%fused_computation.32 | convolution fusion | flops 10871635968 | bytes 28901376 | tf_op jit(solution)/shard_map/dot_general | solution.py:16
  50.4 22.8 %add_convert_fusion = bf16[2048,2304]{1,0:T(8,128)(2,1)} fusion(f32[2048,2304]{1,0:T(8,128)} %fusion.21, bf16[2304,1152]{1,0:T(8,128)(2,1)} %param.12, f32[2048,1152]{1,0:T(8,128)} %get-tuple-element.9, bf16[2048,1152]{1,0:T(8,128)(2,1)} %param.9), kind=kOutput, calls=%fused_computation | convolution fusion | flops 10907025408 | bytes 47775744 | tf_op jit(solution)/shard_map/dot_general | solution.py:16
  73.2 0.1 all-reduce.2.cloned.1.call-update
  73.2 17.1 %fusion.1 = bf16[2304,1152]{0,1:T(8,128)(2,1)} fusion(bf16[2048,1152]{1,0:T(8,128)(2,1)} %get-tuple-element.8, bf16[2048,2304]{1,0:T(8,128)(2,1)} %param.7), kind=kOutput, calls=%fused_computation.12 | convolution fusion | flops 10874290176 | bytes 19464192 | tf_op jit(solution)/shard_map/dot_general | solution.py:18
  90.4 8.5 %copy.11 = bf16[2304,1152]{1,0:T(8,128)(2,1)} copy(bf16[2304,1152]{0,1:T(8,128)(2,1)} %fusion.1) | data formatting | bytes 10616832
  98.9 18.9 %fusion.2 = bf16[2304,1152]{0,1:T(8,128)(2,1)} fusion(bf16[2048,2304]{1,0:T(8,128)(2,1)} %param.7, f32[2048,1152]{1,0:T(8,128)} %get-tuple-element.9, bf16[2048,1152]{1,0:T(8,128)(2,1)} %param.9), kind=kOutput, calls=%fused_computation.13 | convolution fusion | flops 10900242432 | bytes 28901376 | tf_op jit(solution)/shard_map/dot_general | solution.py:19
  117.8 8.5 %copy.12 = bf16[2304,1152]{1,0:T(8,128)(2,1)} copy(bf16[2304,1152]{0,1:T(8,128)(2,1)} %fusion.2) | data formatting | bytes 10616832
  126.4 18.8 %convolution_convert_fusion = bf16[1152,2304]{1,0:T(8,128)(2,1)} fusion(bf16[2048,2304]{1,0:T(8,128)(2,1)} %param.8, bf16[2048,1152]{1,0:T(8,128)(2,1)} %param.10, bf16[2048,1152]{1,0:T(8,128)(2,1)} %param.9), kind=kOutput, calls=%fused_computation.9 | convolution fusion | flops 10902601728 | bytes 24182784 | tf_op jit(solution)/shard_map/dot_general | solution.py:20
  145.1 133.7 %all-reduce.2.cloned.1.call-done = bf16[2048,2304]{1,0:T(8,128)(2,1)} async-done(((bf16[2048,2304]{1,0:T(8,128)(2,1)}), bf16[2048,2304]{1,0:T(8,128)(2,1)}) %all-reduce.2.cloned.1.call-update) | async-done | bytes 9437200 | tf_op jit(solution)/shard_map/psum | solution.py:17
  278.8 8.0 %copy.14 = bf16[2048,2304]{1,0:T(8,128)(2,1)} copy(bf16[2048,2304]{1,0:T(8,128)(2,1)} %all-reduce.2.cloned.1.call-done) | data formatting | bytes 18874368
Async XLA Ops:
  7.2 271.6 %all-reduce.2.cloned.1.call-start = ((), (), s32[]{:S(2)}) async-start(), calls=%async_computation | async-start | bytes 18874368 | tf_op jit(solution)/shard_map/psum | solution.py:17
  7.2 26.2 %copy-start = (bf16[2304,1152]{1,0:T(8,128)(2,1)S(1)}, bf16[2304,1152]{1,0:T(8,128)(2,1)}, u32[]{:S(2)}) copy-start(bf16[2304,1152]{1,0:T(8,128)(2,1)} %param.11) | copy-start | bytes 15925252
Sparse Core Ops, SparseCore 0:
  73.4 205.3 all-reduce.1
where the time goes:
time: 294 us
  waiting for transfers between devices  134 us (46%)
  matrix products  121 us (41%)
  local copies, waits for them, and re-layouts  25.1 us (9%)
  between operations  14.1 us (5%)
    psum x1, waiting for transfers between devices, step(): dx = lax.psum(term.astype(jnp.bfloat16), 'tp')  134 us
    dot_general x1, matrix products, step(): d_hidden = jnp.dot(dy, w_down.T, preferred_element_type=jnp.float32)  26.2 us
    unnamed x5, local copies, waits for them, and re-layouts  25.1 us
    dot_general x1, matrix products, step(): jnp.dot(d_up, w_up.T, preferred_element_type=jnp.float32)  22.8 us
    dot_general x1, matrix products, step(): dw_up = jnp.dot(x.T, d_up, preferred_element_type=jnp.float32)  18.9 us
    dot_general x1, matrix products, step(): jnp.dot(hidden.astype(jnp.bfloat16).T, dy, preferred_element_type=jnp.flo...  18.8 us
    dot_general x1, matrix products, step(): dw_gate = jnp.dot(x.T, d_gate, preferred_element_type=jnp.float32)  17.1 us
    dot_general x1, matrix products, step(): jnp.dot(d_gate, w_gate.T, preferred_element_type=jnp.float32)  16.9 us
  transfers between devices with their start and end apart: 1, of which 1 were waited for; matrix products, arithmetic and copies ran while one was open for 24% of the time, Pallas kernels for 0%

commit v1 on v0

v1 whole, which is shorter than its diff:
```python
import functools

import jax
import jax.numpy as jnp
from jax import lax
from jax.experimental import pallas as pl
from jax.experimental.pallas import tpu as pltpu
from jax.sharding import PartitionSpec as P

MESH = pl.DeviceIdType.MESH
F32 = jnp.float32
BF16 = jnp.bfloat16
PIECES = 3
TILE = 384


def act(gate, up):
    return jax.nn.gelu(gate) * up


def dot_nt(a, b):
    return lax.dot_general(a, b, (((1,), (1,)), ((), ())), preferred_element_type=F32)


def dot_tn(a, b):
    return lax.dot_general(a, b, (((0,), (0,)), ((), ())), preferred_element_type=F32)


def kernel(
    n,
    x, dy, gate, up, w_gate, w_up, w_down,
    dx, dw_gate, dw_up, dw_down,
    w_gu, w_d, d_gu, hid, dy_v, term, slots, stage,
    row_sem, wd_sem, wgu_sem, x_sem, out_sem, own_sem, rs_send, rs_recv, ag_send, ag_recv,
):
    tokens, width = dy_v.shape
    ff = w_d.shape[0]
    block = tokens // n
    half = block // 2
    piece = width // PIECES
    ff_piece = ff // PIECES
    me = lax.axis_index("tp")
    right, left = lax.rem(me + 1, n), lax.rem(me + n - 1, n)
    peers = (right, left)

    def rows_of(side, step):
        if side == 0:
            return pl.ds(pl.multiple_of(lax.rem(me - step + 2 * n, n) * block, block), half)
        return pl.ds(pl.multiple_of(lax.rem(me + step + n, n) * block + half, half), half)

    def held(side, step):
        return pl.ds(pl.multiple_of(step * block + side * half, half), half)

    def row_loads(step):
        parity = lax.rem(step, 2)
        copies = []
        for side in range(2):
            src, dst = rows_of(side, step), held(side, step)
            pairs = (
                (dy.at[src, :], dy_v.at[dst, :]),
                (gate.at[src, :], d_gu.at[dst, pl.ds(0, ff)]),
                (up.at[src, :], d_gu.at[dst, pl.ds(ff, ff)]),
            )
            for i, (a, b) in enumerate(pairs):
                copies.append(pltpu.make_async_copy(a, b, row_sem.at[parity, side * 3 + i]))
        return copies

    def wd_load(i):
        rows = pl.ds(i * ff_piece, ff_piece)
        return pltpu.make_async_copy(w_down.at[rows, :], w_d.at[rows, :], wd_sem.at[i])

    def wgu_loads(i):
        rows = pl.ds(i * piece, piece)
        return [
            pltpu.make_async_copy(w.at[rows, :], w_gu.at[rows, pl.ds(j * ff, ff)], wgu_sem.at[i, j])
            for j, w in enumerate((w_gate, w_up))
        ]

    def x_load(side, step):
        return pltpu.make_async_copy(x.at[rows_of(side, step), :], w_gu.at[held(side, step), :], x_sem.at[step, side])

    def rs_copy(side, step, c):
        return pltpu.make_async_remote_copy(
            src_ref=slots.at[side, step, c],
            dst_ref=slots.at[side, step + 1, c],
            send_sem=rs_send.at[side, step, c],
            recv_sem=rs_recv.at[side, step + 1, c],
            device_id={"tp": peers[side]},
            device_id_type=MESH,
        )

    def columns(c):
        return pl.ds(pl.multiple_of(c * piece, piece), piece)

    def ag_rows(side, hop):
        return rows_of(side, hop + n - 1)

    def ag_copy(side, hop, c, first):
        place = dx.at[ag_rows(side, hop), columns(c)]
        return pltpu.make_async_remote_copy(
            src_ref=slots.at[side, n - 1, c] if first else place,
            dst_ref=place,
            send_sem=ag_send.at[side, hop, c],
            recv_sem=ag_recv.at[side, hop, c],
            device_id={"tp": peers[side]},
            device_id_type=MESH,
        )

    def own_copy(side, c):
        return pltpu.make_async_copy(
            slots.at[side, n - 1, c], dx.at[ag_rows(side, 0), columns(c)], own_sem.at[side, c]
        )

    barrier = pltpu.get_barrier_semaphore()
    for peer in peers:
        pl.semaphore_signal(barrier, inc=1, device_id={"tp": peer}, device_id_type=MESH)
    for copy in row_loads(0):
        copy.start()
    for i in range(PIECES):
        wd_load(i).start()
    for i in range(PIECES):
        for copy in wgu_loads(i):
            copy.start()
    pl.semaphore_wait(barrier, 2)

    def rs_step(step, _):
        for copy in row_loads(step):
            copy.wait()
        rows = pl.ds(pl.multiple_of(step * block, block), block)
        for i in range(PIECES):
            @pl.when(step == 0)
            def _():
                wd_load(i).wait()

            low, high = pl.ds(i * ff_piece, ff_piece), pl.ds(ff + i * ff_piece, ff_piece)
            d_hidden = dot_nt(dy_v[rows, :], w_d[low, :])
            hidden, back = jax.vjp(act, d_gu[rows, low].astype(F32), d_gu[rows, high].astype(F32))
            d_gate, d_up = back(d_hidden)
            hid[rows, low] = hidden.astype(BF16)
            d_gu[rows, low] = d_gate.astype(BF16)
            d_gu[rows, high] = d_up.astype(BF16)

        @pl.when(step < n - 1)
        def _():
            for copy in row_loads(step + 1):
                copy.start()

        for c in range(PIECES):
            @pl.when(step == 0)
            def _():
                for copy in wgu_loads(c):
                    copy.wait()

            part = dot_nt(d_gu[rows, :], w_gu[c * piece : (c + 1) * piece, :])

            @pl.when(step == 0)
            def _():
                for side in range(2):
                    slots[side, 0, c] = part[side * half : (side + 1) * half].astype(BF16)
                for side in range(2):
                    rs_copy(side, 0, c).start()

            @pl.when(step > 0)
            def _():
                term[c] = part

        @pl.when(step == n - 1)
        def _():
            for s in range(n):
                for side in range(2):
                    x_load(side, s).start()

        @pl.when(step > 0)
        def _():
            for c in range(PIECES):
                for side in range(2):
                    rs_copy(side, step - 1, c).wait_recv()
                    total = slots[side, step, c].astype(F32) + term[c, side * half : (side + 1) * half, :]
                    slots[side, step, c] = total.astype(BF16)

                @pl.when(step < n - 1)
                def _():
                    for side in range(2):
                        rs_copy(side, step, c).start()

                @pl.when(step == n - 1)
                def _():
                    for side in range(2):
                        ag_copy(side, 0, c, True).start()
                        own_copy(side, c).start()

        return 0

    lax.fori_loop(0, n, rs_step, 0)

    down_tiles = ff // TILE
    up_tiles = width // TILE
    down_units = down_tiles * (width // ff)
    units = down_units + 2 * up_tiles

    def out_copy(unit):
        slot = lax.rem(unit, 2)
        return pltpu.make_async_copy(stage.at[slot], dw_gate.at[pl.ds(0, TILE), :], out_sem.at[slot])

    def work(unit):
        slot = lax.rem(unit, 2)

        @pl.when(unit >= 2)
        def _():
            out_copy(unit).wait()

        @pl.when(unit < down_units)
        def _():
            row = pl.ds(pl.multiple_of(lax.rem(unit, down_tiles) * TILE, TILE), TILE)
            col = pl.ds(pl.multiple_of(lax.div(unit, down_tiles) * ff, ff), ff)
            stage[slot] = dot_tn(hid[:, row], dy_v[:, col]).astype(BF16)
            pltpu.make_async_copy(stage.at[slot], dw_down.at[row, col], out_sem.at[slot]).start()

        @pl.when(unit == down_units)
        def _():
            for s in range(n):
                for side in range(2):
                    x_load(side, s).wait()

        @pl.when(unit >= down_units)
        def _():
            which = lax.div(unit - down_units, up_tiles)
            row = pl.ds(pl.multiple_of(lax.rem(unit - down_units, up_tiles) * TILE, TILE), TILE)
            col = pl.ds(pl.multiple_of(which * ff, ff), ff)
            stage[slot] = dot_tn(w_gu[pl.ds(0, tokens), row], d_gu[:, col]).astype(BF16)
            for i, out in enumerate((dw_gate, dw_up)):
                @pl.when(which == i)
                def _():
                    pltpu.make_async_copy(stage.at[slot], out.at[row, :], out_sem.at[slot]).start()

    def ag_step(turn, _):
        @pl.when(turn < units)
        def _():
            work(turn)

        hop, c = lax.div(turn, PIECES), lax.rem(turn, PIECES)
        for side in range(2):
            ag_copy(side, hop, c, False).wait_recv()

            @pl.when(hop < n - 2)
            def _():
                ag_copy(side, hop + 1, c, False).start()

        return 0

    turns = (n - 1) * PIECES
    assert units <= turns and width == 2 * ff and tokens <= width
    lax.fori_loop(0, turns, ag_step, 0)

    for unit in (units - 2, units - 1):
        out_copy(unit).wait()

    def sends(hop, _):
        for side in range(2):
            for c in range(PIECES):
                rs_copy(side, hop, c).wait_send()
                ag_copy(side, hop, c, False).wait_send()
        return 0

    lax.fori_loop(0, n - 1, sends, 0)
    for side in range(2):
        for c in range(PIECES):
            own_copy(side, c).wait()


def solution(mesh):
    n = mesh.shape["tp"]

    def step(x, dy, gate, up, w_gate, w_up, w_down):
        tokens, width = x.shape
        ff = gate.shape[1]
        block, half, piece = tokens // n, tokens // n // 2, width // PIECES
        hbm = pl.BlockSpec(memory_space=pl.ANY)
        return pl.pallas_call(
            functools.partial(kernel, n),
            out_shape=[jax.ShapeDtypeStruct(a.shape, BF16) for a in (x, w_gate, w_up, w_down)],
            in_specs=[hbm] * 7,
            out_specs=[hbm] * 4,
            scratch_shapes=[
                pltpu.VMEM((width, 2 * ff), BF16),
                pltpu.VMEM((ff, width), BF16),
                pltpu.VMEM((tokens, 2 * ff), BF16),
                pltpu.VMEM((tokens, ff), BF16),
                pltpu.VMEM((tokens, width), BF16),
                pltpu.VMEM((PIECES, block, piece), F32),
                pltpu.VMEM((2, n, PIECES, half, piece), BF16),
                pltpu.VMEM((2, TILE, ff), BF16),
                pltpu.SemaphoreType.DMA((2, 6)),
                pltpu.SemaphoreType.DMA((PIECES,)),
                pltpu.SemaphoreType.DMA((PIECES, 2)),
                pltpu.SemaphoreType.DMA((n, 2)),
                pltpu.SemaphoreType.DMA((2,)),
                pltpu.SemaphoreType.DMA((2, PIECES)),
                pltpu.SemaphoreType.DMA((2, n, PIECES)),
                pltpu.SemaphoreType.DMA((2, n, PIECES)),
                pltpu.SemaphoreType.DMA((2, n, PIECES)),
                pltpu.SemaphoreType.DMA((2, n, PIECES)),
            ],
            compiler_params=pltpu.CompilerParams(
                collective_id=0, has_side_effects=True, vmem_limit_bytes=67_043_328
            ),
        )(x, dy, gate, up, w_gate, w_up, w_down)

    tokens, columns, rows = P("dp", None), P(None, "tp"), P("tp", None)
    return jax.shard_map(
        step,
        mesh=mesh,
        in_specs=(tokens, tokens, P("dp", "tp"), P("dp", "tp"), columns, columns, rows),
        out_specs=(tokens, P("dp", "tp"), P("dp", "tp"), P(("dp", "tp"), None)),
        check_vma=False,
    )
```

time: 294 us -> 217 us (0.74)
  Pallas kernels: 0 us -> 197 us
  waiting for transfers between devices: 134 us -> 0 us
  matrix products: 121 us -> 0 us
  between operations: 14.1 us -> 0.65 us
  local copies, waits for them, and re-layouts: 25.1 us -> 19.1 us
    pallas_call x0 -> x1, Pallas kernels: none -> 197 us  [step(): pl.pallas_call(functools.partial(kernel, n), out_shape=[jax.ShapeDtypeStr...]
    psum x1 -> x0, waiting for transfers between devices: 134 us -> none  [step(): dx = lax.psum(term.astype(jnp.bfloat16), 'tp')]
    dot_general x6 -> x0, matrix products: 121 us -> none  [the longest x1 26.2 us: step(): d_hidden = jnp.dot(dy, w_down.T, preferred_element_type=jnp.float32)]
    unnamed x5 -> x10, local copies, waits for them, and re-layouts: 25.1 us -> 19.1 us
  transfers between devices with their start and end apart: 1 -> 0, of which waited for: 1 -> 0; matrix products, arithmetic and copies ran while one was open for 24% -> 0% of each run, Pallas kernels for 0% -> 0%
where the time goes in v1:
time: 217 us
  Pallas kernels  197 us (91%)
  local copies, waits for them, and re-layouts  19.1 us (9%)
    pallas_call x1, Pallas kernels, step(): pl.pallas_call(functools.partial(kernel, n), out_shape=[jax.ShapeDtypeStr...  197 us
    unnamed x10, local copies, waits for them, and re-layouts  19.1 us

profile of v1, /device:TPU:21, one launch (start us, length us, event | category | flops | bytes accessed | tf_op | source)
XLA Modules:
  0.0 217.2 jit_solution(15517763216750696373)
XLA Ops:
  0.6 197.4 %shard_map.102 = (bf16[2048,2304]{1,0:T(8,128)(2,1)}, bf16[2304,1152]{1,0:T(8,128)(2,1)}, bf16[2304,1152]{1,0:T(8,128)(2,1)}, bf16[1152,2304]{1,0:T(8,128)(2,1)}) custom-call(bf16[2048,2304]{1,0:T(8,128)(2,1)} %x.1, bf16[2048,2304]{1,0:T(8,128)(2,1)} %dy.1, bf16[2048,1152]{1,0:T(8,128)(2,1)} %gate.1, bf16[2048,1152]{1,0:T(8,128)(2,1)} %up.1, ...), custom_call_target="tpu_custom_call" | custom-call | tf_op jit(solution)/shard_map/pallas_call | solution.py:279
  198.1 0.0 slice-start
  198.1 8.1 %copy.15 = bf16[2048,2304]{1,0:T(8,128)(2,1)} copy(bf16[2048,2304]{1,0:T(8,128)(2,1)} %get-tuple-element.8) | data formatting | bytes 18874368
  206.2 0.0 copy-start
  206.2 0.0 slice-start.1
  206.2 5.8 %copy.16 = bf16[2304,1152]{1,0:T(8,128)(2,1)} copy(bf16[2304,1152]{1,0:T(8,128)(2,1)} %get-tuple-element.9) | data formatting | bytes 10616832
  212.0 0.0 copy-done
  212.0 2.4 %copy.17 = bf16[2304,1152]{1,0:T(8,128)(2,1)} copy(bf16[2304,1152]{1,0:T(8,128)(2,1)S(1)} %copy-done) | data formatting | bytes 10616832
  214.4 0.0 slice-done
  214.4 0.4 slice-done.1
  214.8 2.4 %copy.18 = bf16[1152,2304]{1,0:T(8,128)(2,1)} copy(bf16[1152,2304]{1,0:T(8,128)(2,1)S(1)} %bitcast.1) | data formatting | bytes 10616832
  (1 shorter events, 0.0 us)
Async XLA Ops:
  198.1 16.3 %slice-start = ((s8[5308416]{0:T(1024)(128)(4,1)}), s8[1114112]{0:T(1024)(128)(4,1)S(1)}, s32[]{:S(2)}) async-start(s8[5308416]{0:T(1024)(128)(4,1)} %bitcast), calls=%async_computation | async-start | bytes 2228224
  206.2 5.8 %copy-start = (bf16[2304,1152]{1,0:T(8,128)(2,1)S(1)}, bf16[2304,1152]{1,0:T(8,128)(2,1)}, u32[]{:S(2)}) copy-start(bf16[2304,1152]{1,0:T(8,128)(2,1)} %get-tuple-element.10) | copy-start | bytes 15925252
  206.2 8.6 %slice-start.1 = ((s8[5308416]{0:T(1024)(128)(4,1)}), s8[4194304]{0:T(1024)(128)(4,1)S(1)}, s32[]{:S(2)}) async-start(s8[5308416]{0:T(1024)(128)(4,1)} %bitcast), calls=%async_computation.1 | async-start | bytes 8388608

commit v2 on v1

--- a/solution.py
+++ b/solution.py
@@ -29,7 +29,7 @@
 def kernel(
     n,
     x, dy, gate, up, w_gate, w_up, w_down,
-    dx, dw_gate, dw_up, dw_down,
+    dx, dw_gate, dw_up, dw_down, last_high, last_low,
     w_gu, w_d, d_gu, hid, dy_v, term, slots, stage,
     row_sem, wd_sem, wgu_sem, x_sem, out_sem, own_sem, rs_send, rs_recv, ag_send, ag_recv,
 ):
@@ -57,13 +57,13 @@
         for side in range(2):
             src, dst = rows_of(side, step), held(side, step)
             pairs = (
-                (dy.at[src, :], dy_v.at[dst, :]),
                 (gate.at[src, :], d_gu.at[dst, pl.ds(0, ff)]),
                 (up.at[src, :], d_gu.at[dst, pl.ds(ff, ff)]),
+                (dy.at[src, :], dy_v.at[dst, :]),
             )
             for i, (a, b) in enumerate(pairs):
-                copies.append(pltpu.make_async_copy(a, b, row_sem.at[parity, side * 3 + i]))
-        return copies
+                copies.append((i, pltpu.make_async_copy(a, b, row_sem.at[parity, side * 3 + i])))
+        return [copy for _, copy in sorted(copies, key=lambda pair: pair[0])]
 
     def wd_load(i):
         rows = pl.ds(i * ff_piece, ff_piece)
@@ -95,11 +95,13 @@
     def ag_rows(side, hop):
         return rows_of(side, hop + n - 1)
 
-    def ag_copy(side, hop, c, first):
+    hops = n - 2
+
+    def ag_copy(side, hop, c, first=False, last=False):
         place = dx.at[ag_rows(side, hop), columns(c)]
         return pltpu.make_async_remote_copy(
             src_ref=slots.at[side, n - 1, c] if first else place,
-            dst_ref=place,
+            dst_ref=(last_high, last_low)[side].at[:, columns(c)] if last else place,
             send_sem=ag_send.at[side, hop, c],
             recv_sem=ag_recv.at[side, hop, c],
             device_id={"tp": peers[side]},
@@ -118,52 +120,59 @@
         copy.start()
     for i in range(PIECES):
         wd_load(i).start()
-    for i in range(PIECES):
-        for copy in wgu_loads(i):
-            copy.start()
     pl.semaphore_wait(barrier, 2)
 
     def rs_step(step, _):
-        for copy in row_loads(step):
+        loads = row_loads(step)
+        for copy in loads[:4]:
             copy.wait()
         rows = pl.ds(pl.multiple_of(step * block, block), block)
         for i in range(PIECES):
+            low, high = pl.ds(i * ff_piece, ff_piece), pl.ds(ff + i * ff_piece, ff_piece)
+            g = d_gu[rows, low].astype(F32)
+            value, back = jax.vjp(jax.nn.gelu, g)
+            (slope,) = back(jnp.ones_like(g))
+            term[:, low] = slope
+            term[:, high] = value
+            hid[rows, low] = (value * d_gu[rows, high].astype(F32)).astype(BF16)
+        for copy in loads[4:]:
+            copy.wait()
+        for i in range(PIECES):
             @pl.when(step == 0)
             def _():
                 wd_load(i).wait()
+                for copy in wgu_loads(i):
+                    copy.start()
 
             low, high = pl.ds(i * ff_piece, ff_piece), pl.ds(ff + i * ff_piece, ff_piece)
             d_hidden = dot_nt(dy_v[rows, :], w_d[low, :])
-            hidden, back = jax.vjp(act, d_gu[rows, low].astype(F32), d_gu[rows, high].astype(F32))
-            d_gate, d_up = back(d_hidden)
-            hid[rows, low] = hidden.astype(BF16)
-            d_gu[rows, low] = d_gate.astype(BF16)
-            d_gu[rows, high] = d_up.astype(BF16)
+            d_gu[rows, low] = (d_hidden * d_gu[rows, high].astype(F32) * term[:, low]).astype(BF16)
+            d_gu[rows, high] = (d_hidden * term[:, high]).astype(BF16)
+
+        for c in range(PIECES):
+            @pl.when(step == 0)
+            def _():
+                for copy in wgu_loads(c):
+                    copy.wait()
+
+            part = dot_nt(d_gu[rows, :], w_gu[c * piece : (c + 1) * piece, :])
+
+            @pl.when(step == 0)
+            def _():
+                for side in range(2):
+                    slots[side, 0, c] = part[side * half : (side + 1) * half].astype(BF16)
+                for side in range(2):
+                    rs_copy(side, 0, c).start()
+
+            @pl.when(step > 0)
+            def _():
+                term[:, c * piece : (c + 1) * piece] = part
 
         @pl.when(step < n - 1)
         def _():
             for copy in row_loads(step + 1):
                 copy.start()
 
-        for c in range(PIECES):
-            @pl.when(step == 0)
-            def _():
-                for copy in wgu_loads(c):
-                    copy.wait()
-
-            part = dot_nt(d_gu[rows, :], w_gu[c * piece : (c + 1) * piece, :])
-
-            @pl.when(step == 0)
-            def _():
-                for side in range(2):
-                    slots[side, 0, c] = part[side * half : (side + 1) * half].astype(BF16)
-                for side in range(2):
-                    rs_copy(side, 0, c).start()
-
-            @pl.when(step > 0)
-            def _():
-                term[c] = part
-
         @pl.when(step == n - 1)
         def _():
             for s in range(n):
@@ -175,7 +184,7 @@
             for c in range(PIECES):
                 for side in range(2):
                     rs_copy(side, step - 1, c).wait_recv()
-                    total = slots[side, step, c].astype(F32) + term[c, side * half : (side + 1) * half, :]
+                    total = slots[side, step, c].astype(F32) + term[side * half : (side + 1) * half, c * piece : (c + 1) * piece]
                     slots[side, step, c] = total.astype(BF16)
 
                 @pl.when(step < n - 1)
@@ -186,7 +195,7 @@
                 @pl.when(step == n - 1)
                 def _():
                     for side in range(2):
-                        ag_copy(side, 0, c, True).start()
+                        ag_copy(side, 0, c, first=True).start()
                         own_copy(side, c).start()
 
         return 0
@@ -240,15 +249,19 @@
 
         hop, c = lax.div(turn, PIECES), lax.rem(turn, PIECES)
         for side in range(2):
-            ag_copy(side, hop, c, False).wait_recv()
-
-            @pl.when(hop < n - 2)
-            def _():
-                ag_copy(side, hop + 1, c, False).start()
+            ag_copy(side, hop, c).wait_recv()
+
+            @pl.when(hop < hops - 2)
+            def _():
+                ag_copy(side, hop + 1, c).start()
+
+            @pl.when(hop == hops - 2)
+            def _():
+                ag_copy(side, hop + 1, c, last=True).start()
 
         return 0
 
-    turns = (n - 1) * PIECES
+    turns = hops * PIECES
     assert units <= turns and width == 2 * ff and tokens <= width
     lax.fori_loop(0, turns, ag_step, 0)
 
@@ -259,13 +272,49 @@
         for side in range(2):
             for c in range(PIECES):
                 rs_copy(side, hop, c).wait_send()
-                ag_copy(side, hop, c, False).wait_send()
+
+                @pl.when(hop < hops)
+                def _():
+                    ag_copy(side, hop, c).wait_send()
+
         return 0
 
     lax.fori_loop(0, n - 1, sends, 0)
     for side in range(2):
         for c in range(PIECES):
             own_copy(side, c).wait()
+
+
+def outputs(
+    n, dx_in, dw_gate_in, dw_up_in, dw_down_in, last_high, last_low, dx, dw_gate, dw_up, dw_down, wide, narrow, sems
+):
+    half = last_high.shape[0]
+    block = 2 * half
+    me = lax.axis_index("tp")
+    jobs = []
+    for i in range(n - 1):
+        for side, last in enumerate((last_high, last_low)):
+            place = lax.rem(me + 1 - i + n, n) if side == 0 else lax.rem(me - 1 + i + n, n)
+            rows = pl.ds(pl.multiple_of(place * block + side * half, half), half)
+            jobs.append((dx_in.at[rows, :] if i < n - 2 else last, wide, dx.at[rows, :]))
+    for a, b, buffer in ((dw_down_in, dw_down, wide), (dw_gate_in, dw_gate, narrow), (dw_up_in, dw_up, narrow)):
+        step = buffer.shape[1]
+        for i in range(a.shape[0] // step):
+            rows = pl.ds(i * step, step)
+            jobs.append((a.at[rows, :], buffer, b.at[rows, :]))
+    used = {id(wide): 0, id(narrow): 0}
+    pairs = []
+    for k, (src, buffer, dst) in enumerate(jobs):
+        spot = buffer.at[used[id(buffer)]]
+        used[id(buffer)] += 1
+        pairs.append((pltpu.make_async_copy(src, spot, sems.at[0, k]), pltpu.make_async_copy(spot, dst, sems.at[1, k])))
+    for load, _ in pairs:
+        load.start()
+    for load, store in pairs:
+        load.wait()
+        store.start()
+    for _, store in pairs:
+        store.wait()
 
 
 def solution(mesh):
@@ -276,18 +325,19 @@
         ff = gate.shape[1]
         block, half, piece = tokens // n, tokens // n // 2, width // PIECES
         hbm = pl.BlockSpec(memory_space=pl.ANY)
-        return pl.pallas_call(
+        results = [jax.ShapeDtypeStruct(a.shape, BF16) for a in (x, w_gate, w_up, w_down)]
+        parts = pl.pallas_call(
             functools.partial(kernel, n),
-            out_shape=[jax.ShapeDtypeStruct(a.shape, BF16) for a in (x, w_gate, w_up, w_down)],
+            out_shape=results + [jax.ShapeDtypeStruct((half, width), BF16)] * 2,
             in_specs=[hbm] * 7,
-            out_specs=[hbm] * 4,
+            out_specs=[hbm] * 6,
             scratch_shapes=[
                 pltpu.VMEM((width, 2 * ff), BF16),
                 pltpu.VMEM((ff, width), BF16),
                 pltpu.VMEM((tokens, 2 * ff), BF16),
                 pltpu.VMEM((tokens, ff), BF16),
                 pltpu.VMEM((tokens, width), BF16),
-                pltpu.VMEM((PIECES, block, piece), F32),
+                pltpu.VMEM((block, width), F32),
                 pltpu.VMEM((2, n, PIECES, half, piece), BF16),
                 pltpu.VMEM((2, TILE, ff), BF16),
                 pltpu.SemaphoreType.DMA((2, 6)),
@@ -305,6 +355,28 @@
                 collective_id=0, has_side_effects=True, vmem_limit_bytes=67_043_328
             ),
         )(x, dy, gate, up, w_gate, w_up, w_down)
+        last_high, last_low = parts[4:]
+        high = lax.ppermute(last_high, "tp", [(i, (i + 1) % n) for i in range(n)])
+        low = lax.ppermute(last_low, "tp", [(i, (i - 1) % n) for i in range(n)])
+        wide = 2 * (n - 1) + ff // half
+        narrow = 2 * (width // block)
+        dx, dw_gate, dw_up, dw_down = pl.pallas_call(
+            functools.partial(outputs, n),
+            out_shape=results,
+            in_specs=[hbm] * 6,
+            out_specs=[hbm] * 4,
+            scratch_shapes=[
+                pltpu.VMEM((wide, half, width), BF16),
+                pltpu.VMEM((narrow, block, ff), BF16),
+                pltpu.SemaphoreType.DMA((2, wide + narrow)),
+            ],
+            cost_estimate=pl.CostEstimate(flops=2**34, bytes_accessed=2**25, transcendentals=0),
+            compiler_params=pltpu.CompilerParams(has_side_effects=True),
+        )(*parts)
+        me = lax.axis_index("tp")
+        dx = lax.dynamic_update_slice(dx, high, (lax.rem(me + 2, n) * block, 0))
+        dx = lax.dynamic_update_slice(dx, low, (lax.rem(me - 2 + n, n) * block + half, 0))
+        return dx, dw_gate, dw_up, dw_down
 
     tokens, columns, rows = P("dp", None), P(None, "tp"), P("tp", None)
     return jax.shard_map(

time: 217 us -> 204 us (0.940)
  local copies, waits for them, and re-layouts: 19.1 us -> 1.71 us
  starting transfers between devices: 0 us -> 2.76 us
    unnamed x10 -> x0, local copies, waits for them, and re-layouts: 19.1 us -> none
    ppermute x0 -> x2, starting transfers between devices: none -> 2.76 us  [the longest x1 2.65 us: step(): low = lax.ppermute(last_low, 'tp', [(i, (i - 1) % n) for i in range(n)])]
    pallas_call x1 -> x2, Pallas kernels: 197 us -> 199 us  [the longest x1 182 us: step(): pl.pallas_call(functools.partial(kernel, n), out_shape=results + [jax.Sha...]
  transfers between devices with their start and end apart: 0 -> 2, of which waited for: 0 -> 0; matrix products, arithmetic and copies ran while one was open for 0% -> 0% of each run, Pallas kernels for 0% -> 8%
where the time goes in v2:
time: 204 us
  Pallas kernels  199 us (98%)
  starting transfers between devices  2.76 us (1%)
    pallas_call x1, Pallas kernels, step(): pl.pallas_call(functools.partial(kernel, n), out_shape=results + [jax.Sha...  182 us
    pallas_call x1, Pallas kernels, step(): pl.pallas_call(functools.partial(outputs, n), out_shape=results, in_specs...  16.9 us
  transfers between devices with their start and end apart: 2, of which 0 were waited for; matrix products, arithmetic and copies ran while one was open for 0% of the time, Pallas kernels for 8%

profile of v2, /device:TPU:21, one launch (start us, length us, event | category | flops | bytes accessed | tf_op | source)
XLA Modules:
  0.0 204.3 jit_solution(15382037114372208447)
XLA Ops:
  0.6 182.2 %shard_map.102 = (bf16[2048,2304]{1,0:T(8,128)(2,1)}, bf16[2304,1152]{1,0:T(8,128)(2,1)}, bf16[2304,1152]{1,0:T(8,128)(2,1)}, bf16[1152,2304]{1,0:T(8,128)(2,1)}...) custom-call(bf16[2048,2304]{1,0:T(8,128)(2,1)} %x.1, bf16[2048,2304]{1,0:T(8,128)(2,1)} %dy.1, ...), custom_call_target="tpu_custom_call" | custom-call | tf_op jit(solution)/shard_map/pallas_call | solution.py:329
  182.8 0.1 collective-permute-start
  183.0 2.7 %collective-permute-start.1 = (bf16[128,2304]{1,0:T(8,128)(2,1)}, bf16[128,2304]{1,0:T(8,128)(2,1)S(1)}, u32[]{:S(2)}, u32[]{:S(2)}) collective-permute-start(bf16[128,2304]{1,0:T(8,128)(2,1)} %get-tuple-element.19.last_low), channel_id=1, source_target_pairs={{0,7},{1,0},{2,1},{3,2},{4,3},{5,4},{6,5},{7,6},{8,15},{9,8},{10,9... | collective-permute-start | bytes 1769480 | tf_op jit(solution)/shard_map/ppermute | solution.py:360
  185.6 16.9 %shard_map.103 = (bf16[2048,2304]{1,0:T(8,128)(2,1)}, bf16[2304,1152]{1,0:T(8,128)(2,1)}, bf16[2304,1152]{1,0:T(8,128)(2,1)}, bf16[1152,2304]{1,0:T(8,128)(2,1)}) custom-call(bf16[2048,2304]{1,0:T(8,128)(2,1)} %get-tuple-element.14.dx_in, bf16[2304,1152]{1,0:T(8,128)(2,1)} %get-tuple-element.15.dw_gate_in, bf16[2304,1152]{1,0:T(8,128)(2,1)} %get-tuple-element.16.dw_up_in, ...), custom_call_target="tpu_custom_call" | custom-call | flops 17179869184 | bytes 33554432 | tf_op jit(solution)/shard_map/pallas_call | solution.py:363
  202.6 0.0 collective-permute-done
  202.6 0.9 constant_dynamic-update-slice_fusion.1
  203.4 0.0 collective-permute-done.1
  203.4 0.9 constant_dynamic-update-slice_fusion
Async XLA Ops:
  182.8 19.7 %collective-permute-start = (bf16[128,2304]{1,0:T(8,128)(2,1)}, bf16[128,2304]{1,0:T(8,128)(2,1)S(1)}, u32[]{:S(2)}, u32[]{:S(2)}) collective-permute-start(bf16[128,2304]{1,0:T(8,128)(2,1)} %get-tuple-element.18.last_high), channel_id=1, source_target_pairs={{0,1},{1,2},{2,3},{3,4},{4,5},{5,6},{6,7},{7,0},{8,9},{9,10},{10,1... | collective-permute-start | bytes 1769480 | tf_op jit(solution)/shard_map/ppermute | solution.py:359
  183.0 20.5 %collective-permute-start.1 = (bf16[128,2304]{1,0:T(8,128)(2,1)}, bf16[128,2304]{1,0:T(8,128)(2,1)S(1)}, u32[]{:S(2)}, u32[]{:S(2)}) collective-permute-start(bf16[128,2304]{1,0:T(8,128)(2,1)} %get-tuple-element.19.last_low), channel_id=1, source_target_pairs={{0,7},{1,0},{2,1},{3,2},{4,3},{5,4},{6,5},{7,6},{8,15},{9,8},{10,9... | collective-permute-start | bytes 1769480 | tf_op jit(solution)/shard_map/ppermute | solution.py:360

commit v3 on v2

v3 whole, which is shorter than its diff:
```python
import functools

import jax
import jax.numpy as jnp
from jax import lax
from jax.experimental import pallas as pl
from jax.experimental.pallas import tpu as pltpu
from jax.sharding import PartitionSpec as P

MESH = pl.DeviceIdType.MESH
F32 = jnp.float32
BF16 = jnp.bfloat16
PIECES = 3
FIRST = 3
TILE = 384


def dot_nt(a, b):
    return lax.dot_general(a, b, (((1,), (1,)), ((), ())), preferred_element_type=F32)


def dot_tn(a, b):
    return lax.dot_general(a, b, (((0,), (0,)), ((), ())), preferred_element_type=F32)


def kernel(
    n,
    x, dy, gate, up, w_gate, w_up, w_down,
    dx, dw_gate, dw_up, dw_down, last,
    w_gu, w_d, d_gu, hid, dy_v, term, slots, stage,
    row_sem, wd_sem, wgu_sem, x_sem, out_sem, own_sem, rs_send, rs_recv, ag_send, ag_recv,
):
    tokens, width = dy_v.shape
    ff = w_d.shape[0]
    block = tokens // n
    piece = width // PIECES
    first = piece // FIRST
    ff_piece = ff // PIECES
    me = lax.axis_index("tp")
    ahead = 1 - 2 * lax.rem(lax.axis_index("dp"), 2)
    peer = lax.rem(me + ahead + n, n)
    behind = lax.rem(me - ahead + n, n)
    hops = n - 2

    def block_rows(step):
        return pl.ds(pl.multiple_of(lax.rem(me - ahead * step + 2 * n, n) * block, block), block)

    def held(step):
        return pl.ds(pl.multiple_of(step * block, block), block)

    def row_loads(step):
        parity = lax.rem(step, 2)
        src, dst = block_rows(step), held(step)
        pairs = (
            (gate.at[src, :], d_gu.at[dst, pl.ds(0, ff)]),
            (up.at[src, :], d_gu.at[dst, pl.ds(ff, ff)]),
            (dy.at[src, :], dy_v.at[dst, :]),
        )
        return [pltpu.make_async_copy(a, b, row_sem.at[parity, i]) for i, (a, b) in enumerate(pairs)]

    def wd_load(i):
        rows = pl.ds(i * ff_piece, ff_piece)
        return pltpu.make_async_copy(w_down.at[rows, :], w_d.at[rows, :], wd_sem.at[i])

    tiles = [(i * first, first) for i in range(FIRST)] + [(c * piece, piece) for c in range(1, PIECES)]

    def wgu_loads(i):
        rows = pl.ds(*tiles[i])
        return [
            pltpu.make_async_copy(w.at[rows, :], w_gu.at[rows, pl.ds(j * ff, ff)], wgu_sem.at[i, j])
            for j, w in enumerate((w_gate, w_up))
        ]

    def x_load(step):
        return pltpu.make_async_copy(x.at[block_rows(step), :], w_gu.at[held(step), :], x_sem.at[step])

    def rs_copy(step, c, part=None):
        part = slice(None) if part is None else part
        return pltpu.make_async_remote_copy(
            src_ref=slots.at[step, c, :, part],
            dst_ref=slots.at[step + 1, c, :, part],
            send_sem=rs_send.at[step, c],
            recv_sem=rs_recv.at[step + 1, c],
            device_id={"tp": peer},
            device_id_type=MESH,
        )

    def columns(c):
        return pl.ds(pl.multiple_of(c * piece, piece), piece)

    def ag_copy(hop, c, own=False, final=False):
        place = dx.at[block_rows(hop + n - 1), columns(c)]
        return pltpu.make_async_remote_copy(
            src_ref=slots.at[n - 1, c] if own else place,
            dst_ref=last.at[:, columns(c)] if final else place,
            send_sem=ag_send.at[hop, c],
            recv_sem=ag_recv.at[hop, c],
            device_id={"tp": peer},
            device_id_type=MESH,
        )

    def own_copy(c):
        return pltpu.make_async_copy(slots.at[n - 1, c], dx.at[block_rows(n - 1), columns(c)], own_sem.at[c])

    barrier = pltpu.get_barrier_semaphore()
    for other in (peer, behind):
        pl.semaphore_signal(barrier, inc=1, device_id={"tp": other}, device_id_type=MESH)
    for copy in row_loads(0):
        copy.start()
    for i in range(PIECES):
        wd_load(i).start()
    pl.semaphore_wait(barrier, 2)

    def rs_step(step, _):
        loads = row_loads(step)
        for copy in loads[:2]:
            copy.wait()
        rows = held(step)
        for i in range(PIECES):
            low, high = pl.ds(i * ff_piece, ff_piece), pl.ds(ff + i * ff_piece, ff_piece)
            g = d_gu[rows, low].astype(F32)
            value, back = jax.vjp(jax.nn.gelu, g)
            (slope,) = back(jnp.ones_like(g))
            term[:, low] = slope
            term[:, high] = value
            hid[rows, low] = (value * d_gu[rows, high].astype(F32)).astype(BF16)
        loads[2].wait()
        for i in range(PIECES):
            @pl.when(step == 0)
            def _():
                wd_load(i).wait()
                for tile in ((0, 1), (2,), (3,))[i]:
                    for copy in wgu_loads(tile):
                        copy.start()

            low, high = pl.ds(i * ff_piece, ff_piece), pl.ds(ff + i * ff_piece, ff_piece)
            d_hidden = dot_nt(dy_v[rows, :], w_d[low, :])
            d_gu[rows, low] = (d_hidden * d_gu[rows, high].astype(F32) * term[:, low]).astype(BF16)
            d_gu[rows, high] = (d_hidden * term[:, high]).astype(BF16)

        for i, (start, size) in enumerate(tiles):
            @pl.when(step == 0)
            def _():
                for copy in wgu_loads(i):
                    copy.wait()
                if i == 0:
                    for copy in wgu_loads(4):
                        copy.start()

            part = dot_nt(d_gu[rows, :], w_gu[start : start + size, :])

            @pl.when(step == 0)
            def _():
                c = start // piece
                cols = slice(start - c * piece, start - c * piece + size)
                slots[0, c, :, cols] = part.astype(BF16)
                rs_copy(0, c, cols).start()

            @pl.when(step > 0)
            def _():
                term[:, start : start + size] = part

        @pl.when(step < n - 1)
        def _():
            for copy in row_loads(step + 1):
                copy.start()

        @pl.when(step == n - 1)
        def _():
            for s in range(n):
                x_load(s).start()

        @pl.when(step > 0)
        def _():
            for c in range(PIECES):
                rs_copy(step - 1, c).wait_recv()
                total = slots[step, c].astype(F32) + term[:, c * piece : (c + 1) * piece]
                slots[step, c] = total.astype(BF16)

                @pl.when(step < n - 1)
                def _():
                    rs_copy(step, c).start()

                @pl.when(step == n - 1)
                def _():
                    ag_copy(0, c, own=True).start()
                    own_copy(c).start()

        return 0

    lax.fori_loop(0, n, rs_step, 0)

    down_tiles = ff // TILE
    up_tiles = width // TILE
    down_units = down_tiles * (width // ff)
    units = down_units + 2 * up_tiles

    def out_copy(unit):
        slot = lax.rem(unit, 2)
        return pltpu.make_async_copy(stage.at[slot], dw_gate.at[pl.ds(0, TILE), :], out_sem.at[slot])

    def work(unit):
        slot = lax.rem(unit, 2)

        @pl.when(unit >= 2)
        def _():
            out_copy(unit).wait()

        @pl.when(unit < down_units)
        def _():
            row = pl.ds(pl.multiple_of(lax.rem(unit, down_tiles) * TILE, TILE), TILE)
            col = pl.ds(pl.multiple_of(lax.div(unit, down_tiles) * ff, ff), ff)
            stage[slot] = dot_tn(hid[:, row], dy_v[:, col]).astype(BF16)
            pltpu.make_async_copy(stage.at[slot], dw_down.at[row, col], out_sem.at[slot]).start()

        @pl.when(unit == down_units)
        def _():
            for s in range(n):
                x_load(s).wait()

        @pl.when(unit >= down_units)
        def _():
            which = lax.div(unit - down_units, up_tiles)
            row = pl.ds(pl.multiple_of(lax.rem(unit - down_units, up_tiles) * TILE, TILE), TILE)
            col = pl.ds(pl.multiple_of(which * ff, ff), ff)
            stage[slot] = dot_tn(w_gu[pl.ds(0, tokens), row], d_gu[:, col]).astype(BF16)
            for i, out in enumerate((dw_gate, dw_up)):
                @pl.when(which == i)
                def _():
                    pltpu.make_async_copy(stage.at[slot], out.at[row, :], out_sem.at[slot]).start()

    def ag_step(turn, _):
        @pl.when(turn < units)
        def _():
            work(turn)

        hop, c = lax.div(turn, PIECES), lax.rem(turn, PIECES)
        ag_copy(hop, c).wait_recv()

        @pl.when(hop < hops - 2)
        def _():
            ag_copy(hop + 1, c).start()

        @pl.when(hop == hops - 2)
        def _():
            ag_copy(hop + 1, c, final=True).start()

        return 0

    turns = hops * PIECES
    assert units <= turns and width == 2 * ff and tokens <= width
    lax.fori_loop(0, turns, ag_step, 0)

    for unit in (units - 2, units - 1):
        out_copy(unit).wait()

    def sends(hop, _):
        for c in range(PIECES):
            rs_copy(hop, c).wait_send()

            @pl.when(hop < hops)
            def _():
                ag_copy(hop, c).wait_send()

        return 0

    lax.fori_loop(0, n - 1, sends, 0)
    for c in range(PIECES):
        own_copy(c).wait()


def outputs(n, dx_in, dw_gate_in, dw_up_in, dw_down_in, last, dx, dw_gate, dw_up, dw_down, wide, narrow, sems):
    block = last.shape[0]
    me = lax.axis_index("tp")
    ahead = 1 - 2 * lax.rem(lax.axis_index("dp"), 2)
    jobs = []
    for i in range(n - 1):
        rows = pl.ds(pl.multiple_of(lax.rem(me + ahead - ahead * i + n, n) * block, block), block)
        jobs.append((dx_in.at[rows, :] if i < n - 2 else last, wide.at[pl.ds(i * block, block), :], dx.at[rows, :]))
    spot = (n - 1) * block
    for i in range(dw_down.shape[0] // TILE):
        rows = pl.ds(i * TILE, TILE)
        jobs.append((dw_down_in.at[rows, :], wide.at[pl.ds(spot + i * TILE, TILE), :], dw_down.at[rows, :]))
    step = 2 * TILE
    for j, (a, b) in enumerate(((dw_gate_in, dw_gate), (dw_up_in, dw_up))):
        for i in range(b.shape[0] // step):
            rows = pl.ds(i * step, step)
            jobs.append((a.at[rows, :], narrow.at[j, rows, :], b.at[rows, :]))
    loads = [pltpu.make_async_copy(a, v, sems.at[0, k]) for k, (a, v, _) in enumerate(jobs)]
    stores = [pltpu.make_async_copy(v, b, sems.at[1, k]) for k, (_, v, b) in enumerate(jobs)]
    for load in loads:
        load.start()
    for load, store in zip(loads, stores):
        load.wait()
        store.start()
    for store in stores:
        store.wait()


def solution(mesh):
    n, groups = mesh.shape["tp"], mesh.shape["dp"]

    def step(x, dy, gate, up, w_gate, w_up, w_down):
        tokens, width = x.shape
        ff = gate.shape[1]
        block, piece = tokens // n, width // PIECES
        hbm = pl.BlockSpec(memory_space=pl.ANY)
        results = [jax.ShapeDtypeStruct(a.shape, BF16) for a in (x, w_gate, w_up, w_down)]
        parts = pl.pallas_call(
            functools.partial(kernel, n),
            out_shape=results + [jax.ShapeDtypeStruct((block, width), BF16)],
            in_specs=[hbm] * 7,
            out_specs=[hbm] * 5,
            scratch_shapes=[
                pltpu.VMEM((width, 2 * ff), BF16),
                pltpu.VMEM((ff, width), BF16),
                pltpu.VMEM((tokens, 2 * ff), BF16),
                pltpu.VMEM((tokens, ff), BF16),
                pltpu.VMEM((tokens, width), BF16),
                pltpu.VMEM((block, width), F32),
                pltpu.VMEM((n, PIECES, block, piece), BF16),
                pltpu.VMEM((2, TILE, ff), BF16),
                pltpu.SemaphoreType.DMA((2, 3)),
                pltpu.SemaphoreType.DMA((PIECES,)),
                pltpu.SemaphoreType.DMA((FIRST + PIECES - 1, 2)),
                pltpu.SemaphoreType.DMA((n,)),
                pltpu.SemaphoreType.DMA((2,)),
                pltpu.SemaphoreType.DMA((PIECES,)),
                pltpu.SemaphoreType.DMA((n, PIECES)),
                pltpu.SemaphoreType.DMA((n, PIECES)),
                pltpu.SemaphoreType.DMA((n, PIECES)),
                pltpu.SemaphoreType.DMA((n, PIECES)),
            ],
            compiler_params=pltpu.CompilerParams(
                collective_id=0, has_side_effects=True, vmem_limit_bytes=67_043_328
            ),
        )(x, dy, gate, up, w_gate, w_up, w_down)
        ring = [(d * n + i, d * n + (i + 1 - 2 * (d % 2)) % n) for d in range(groups) for i in range(n)]
        final = lax.ppermute(parts[4], ("dp", "tp"), ring)
        dx, dw_gate, dw_up, dw_down = pl.pallas_call(
            functools.partial(outputs, n),
            out_shape=results,
            in_specs=[hbm] * 5,
            out_specs=[hbm] * 4,
            scratch_shapes=[
                pltpu.VMEM(((n - 1) * block + ff, width), BF16),
                pltpu.VMEM((2, width, ff), BF16),
                pltpu.SemaphoreType.DMA((2, n - 1 + ff // TILE + width // TILE)),
            ],
            cost_estimate=pl.CostEstimate(flops=2**34, bytes_accessed=2**25, transcendentals=0),
            compiler_params=pltpu.CompilerParams(has_side_effects=True),
        )(*parts)
        me = lax.axis_index("tp")
        ahead = 1 - 2 * lax.rem(lax.axis_index("dp"), 2)
        dx = lax.dynamic_update_slice(dx, final, (lax.rem(me + 2 * ahead + n, n) * block, 0))
        return dx, dw_gate, dw_up, dw_down

    tokens, columns, rows = P("dp", None), P(None, "tp"), P("tp", None)
    return jax.shard_map(
        step,
        mesh=mesh,
        in_specs=(tokens, tokens, P("dp", "tp"), P("dp", "tp"), columns, columns, rows),
        out_specs=(tokens, P("dp", "tp"), P("dp", "tp"), P(("dp", "tp"), None)),
        check_vma=False,
    )
```

time: 204 us -> 203 us (level)
  transfers between devices with their start and end apart: 2 -> 1, of which waited for: 0 -> 0; matrix products, arithmetic and copies ran while one was open for 0% -> 0% of each run, Pallas kernels for 8% -> 8%
where the time goes in v3:
time: 203 us; the launch traced here: 202 us
  Pallas kernels  197 us (97%)
  starting transfers between devices  3.31 us (2%)
    pallas_call x1, Pallas kernels, step(): pl.pallas_call(functools.partial(kernel, n), out_shape=results + [jax.Sha...  180 us
    pallas_call x1, Pallas kernels, step(): pl.pallas_call(functools.partial(outputs, n), out_shape=results, in_specs...  16.8 us
  transfers between devices with their start and end apart: 1, of which 0 were waited for; matrix products, arithmetic and copies ran while one was open for 0% of the time, Pallas kernels for 8%

profile of v3, /device:TPU:21, one launch (start us, length us, event | category | flops | bytes accessed | tf_op | source)
XLA Modules:
  0.0 202.4 jit_solution(16509232498930051141)
XLA Ops:
  0.6 180.5 %shard_map.102 = (bf16[2048,2304]{1,0:T(8,128)(2,1)}, bf16[2304,1152]{1,0:T(8,128)(2,1)}, bf16[2304,1152]{1,0:T(8,128)(2,1)}, bf16[1152,2304]{1,0:T(8,128)(2,1)}, bf16[256,2304]{1,0:T(8,128)(2,1)}) custom-call(bf16[2048,2304]{1,0:T(8,128)(2,1)} %x.1, bf16[2048,2304]{1,0:T(8,128)(2,1)} %dy.1, bf16[2048,1152]{1,0:T(8,128)(2,1)} %gate.1, ...), custom_call_target="tpu_custom_call" | custom-call | tf_op jit(solution)/shard_map/pallas_call | solution.py:309
  181.1 3.3 %collective-permute-start = (bf16[256,2304]{1,0:T(8,128)(2,1)}, bf16[256,2304]{1,0:T(8,128)(2,1)S(1)}, u32[]{:S(2)}, u32[]{:S(2)}) collective-permute-start(bf16[256,2304]{1,0:T(8,128)(2,1)} %get-tuple-element.17.last), channel_id=1, source_target_pairs={{0,1},{1,2},{2,3},{3,4},{4,5},{5,6},{6,7},{7,0},{8,15},{9,8},{10,9... | collective-permute-start | bytes 3538952 | tf_op jit(solution)/shard_map/ppermute | solution.py:339
  184.4 16.8 %shard_map.103 = (bf16[2048,2304]{1,0:T(8,128)(2,1)}, bf16[2304,1152]{1,0:T(8,128)(2,1)}, bf16[2304,1152]{1,0:T(8,128)(2,1)}, bf16[1152,2304]{1,0:T(8,128)(2,1)}) custom-call(bf16[2048,2304]{1,0:T(8,128)(2,1)} %get-tuple-element.13.dx_in, bf16[2304,1152]{1,0:T(8,128)(2,1)} %get-tuple-element.14.dw_gate_in, bf16[2304,1152]{1,0:T(8,128)(2,1)} %get-tuple-element.15.dw_up_in, ...), custom_call_target="tpu_custom_call" | custom-call | flops 17179869184 | bytes 33554432 | tf_op jit(solution)/shard_map/pallas_call | solution.py:340
  201.3 0.0 collective-permute-done
  201.3 1.1 constant_dynamic-update-slice_fusion
Async XLA Ops:
  181.1 20.2 %collective-permute-start = (bf16[256,2304]{1,0:T(8,128)(2,1)}, bf16[256,2304]{1,0:T(8,128)(2,1)S(1)}, u32[]{:S(2)}, u32[]{:S(2)}) collective-permute-start(bf16[256,2304]{1,0:T(8,128)(2,1)} %get-tuple-element.17.last), channel_id=1, source_target_pairs={{0,1},{1,2},{2,3},{3,4},{4,5},{5,6},{6,7},{7,0},{8,15},{9,8},{10,9... | collective-permute-start | bytes 3538952 | tf_op jit(solution)/shard_map/ppermute | solution.py:339

commit v4 on v3

--- a/solution.py
+++ b/solution.py
@@ -10,8 +10,9 @@
 MESH = pl.DeviceIdType.MESH
 F32 = jnp.float32
 BF16 = jnp.bfloat16
-PIECES = 3
-FIRST = 3
+PIECES = 2
+FIRST = 256
+FF_PIECES = 3
 TILE = 384
 
 
@@ -34,8 +35,7 @@
     ff = w_d.shape[0]
     block = tokens // n
     piece = width // PIECES
-    first = piece // FIRST
-    ff_piece = ff // PIECES
+    ff_piece = ff // FF_PIECES
     me = lax.axis_index("tp")
     ahead = 1 - 2 * lax.rem(lax.axis_index("dp"), 2)
     peer = lax.rem(me + ahead + n, n)
@@ -62,7 +62,7 @@
         rows = pl.ds(i * ff_piece, ff_piece)
         return pltpu.make_async_copy(w_down.at[rows, :], w_d.at[rows, :], wd_sem.at[i])
 
-    tiles = [(i * first, first) for i in range(FIRST)] + [(c * piece, piece) for c in range(1, PIECES)]
+    tiles = [(0, FIRST), (FIRST, piece - FIRST)] + [(c * piece, piece) for c in range(1, PIECES)]
 
     def wgu_loads(i):
         rows = pl.ds(*tiles[i])
@@ -107,7 +107,7 @@
         pl.semaphore_signal(barrier, inc=1, device_id={"tp": other}, device_id_type=MESH)
     for copy in row_loads(0):
         copy.start()
-    for i in range(PIECES):
+    for i in range(FF_PIECES):
         wd_load(i).start()
     pl.semaphore_wait(barrier, 2)
 
@@ -116,7 +116,7 @@
         for copy in loads[:2]:
             copy.wait()
         rows = held(step)
-        for i in range(PIECES):
+        for i in range(FF_PIECES):
             low, high = pl.ds(i * ff_piece, ff_piece), pl.ds(ff + i * ff_piece, ff_piece)
             g = d_gu[rows, low].astype(F32)
             value, back = jax.vjp(jax.nn.gelu, g)
@@ -125,13 +125,12 @@
             term[:, high] = value
             hid[rows, low] = (value * d_gu[rows, high].astype(F32)).astype(BF16)
         loads[2].wait()
-        for i in range(PIECES):
+        for i in range(FF_PIECES):
             @pl.when(step == 0)
             def _():
                 wd_load(i).wait()
-                for tile in ((0, 1), (2,), (3,))[i]:
-                    for copy in wgu_loads(tile):
-                        copy.start()
+                for copy in wgu_loads(i):
+                    copy.start()
 
             low, high = pl.ds(i * ff_piece, ff_piece), pl.ds(ff + i * ff_piece, ff_piece)
             d_hidden = dot_nt(dy_v[rows, :], w_d[low, :])
@@ -143,9 +142,6 @@
             def _():
                 for copy in wgu_loads(i):
                     copy.wait()
-                if i == 0:
-                    for copy in wgu_loads(4):
-                        copy.start()
 
             part = dot_nt(d_gu[rows, :], w_gu[start : start + size, :])
 
@@ -229,10 +225,14 @@
                 def _():
                     pltpu.make_async_copy(stage.at[slot], out.at[row, :], out_sem.at[slot]).start()
 
+    turns = hops * PIECES
+    per_turn = -(-units // turns)
+
     def ag_step(turn, _):
-        @pl.when(turn < units)
-        def _():
-            work(turn)
+        for k in range(per_turn):
+            @pl.when(turn * per_turn + k < units)
+            def _():
+                work(turn * per_turn + k)
 
         hop, c = lax.div(turn, PIECES), lax.rem(turn, PIECES)
         ag_copy(hop, c).wait_recv()
@@ -247,8 +247,7 @@
 
         return 0
 
-    turns = hops * PIECES
-    assert units <= turns and width == 2 * ff and tokens <= width
+    assert FF_PIECES == PIECES + 1 and width == 2 * ff and tokens <= width
     lax.fori_loop(0, turns, ag_step, 0)
 
     for unit in (units - 2, units - 1):
@@ -321,8 +320,8 @@
                 pltpu.VMEM((n, PIECES, block, piece), BF16),
                 pltpu.VMEM((2, TILE, ff), BF16),
                 pltpu.SemaphoreType.DMA((2, 3)),
-                pltpu.SemaphoreType.DMA((PIECES,)),
-                pltpu.SemaphoreType.DMA((FIRST + PIECES - 1, 2)),
+                pltpu.SemaphoreType.DMA((FF_PIECES,)),
+                pltpu.SemaphoreType.DMA((PIECES + 1, 2)),
                 pltpu.SemaphoreType.DMA((n,)),
                 pltpu.SemaphoreType.DMA((2,)),
                 pltpu.SemaphoreType.DMA((PIECES,)),

time: 203 us -> 200 us (0.985)
    pallas_call x1, Pallas kernels: 180 us -> 178 us  [step(): pl.pallas_call(functools.partial(kernel, n), out_shape=results + [jax.Sha...]
where the time goes in v4:
time: 200 us
  Pallas kernels  195 us (98%)
  starting transfers between devices  3.29 us (2%)
    pallas_call x1, Pallas kernels, step(): pl.pallas_call(functools.partial(kernel, n), out_shape=results + [jax.Sha...  178 us
    pallas_call x1, Pallas kernels, step(): pl.pallas_call(functools.partial(outputs, n), out_shape=results, in_specs...  16.8 us
  transfers between devices with their start and end apart: 1, of which 0 were waited for; matrix products, arithmetic and copies ran while one was open for 0% of the time, Pallas kernels for 8%

profile of v4, /device:TPU:21, one launch (start us, length us, event | category | flops | bytes accessed | tf_op | source)
XLA Modules:
  0.0 199.8 jit_solution(16116391165809056078)
XLA Ops:
  0.6 177.9 %shard_map.102 = (bf16[2048,2304]{1,0:T(8,128)(2,1)}, bf16[2304,1152]{1,0:T(8,128)(2,1)}, bf16[2304,1152]{1,0:T(8,128)(2,1)}, bf16[1152,2304]{1,0:T(8,128)(2,1)}, bf16[256,2304]{1,0:T(8,128)(2,1)}) custom-call(bf16[2048,2304]{1,0:T(8,128)(2,1)} %x.1, bf16[2048,2304]{1,0:T(8,128)(2,1)} %dy.1, bf16[2048,1152]{1,0:T(8,128)(2,1)} %gate.1, ...), custom_call_target="tpu_custom_call" | custom-call | tf_op jit(solution)/shard_map/pallas_call | solution.py:308
  178.6 3.3 %collective-permute-start = (bf16[256,2304]{1,0:T(8,128)(2,1)}, bf16[256,2304]{1,0:T(8,128)(2,1)S(1)}, u32[]{:S(2)}, u32[]{:S(2)}) collective-permute-start(bf16[256,2304]{1,0:T(8,128)(2,1)} %get-tuple-element.17.last), channel_id=1, source_target_pairs={{0,1},{1,2},{2,3},{3,4},{4,5},{5,6},{6,7},{7,0},{8,15},{9,8},{10,9... | collective-permute-start | bytes 3538952 | tf_op jit(solution)/shard_map/ppermute | solution.py:338
  181.8 16.8 %shard_map.103 = (bf16[2048,2304]{1,0:T(8,128)(2,1)}, bf16[2304,1152]{1,0:T(8,128)(2,1)}, bf16[2304,1152]{1,0:T(8,128)(2,1)}, bf16[1152,2304]{1,0:T(8,128)(2,1)}) custom-call(bf16[2048,2304]{1,0:T(8,128)(2,1)} %get-tuple-element.13.dx_in, bf16[2304,1152]{1,0:T(8,128)(2,1)} %get-tuple-element.14.dw_gate_in, bf16[2304,1152]{1,0:T(8,128)(2,1)} %get-tuple-element.15.dw_up_in, ...), custom_call_target="tpu_custom_call" | custom-call | flops 17179869184 | bytes 33554432 | tf_op jit(solution)/shard_map/pallas_call | solution.py:339
  198.7 0.0 collective-permute-done
  198.7 1.1 constant_dynamic-update-slice_fusion
Async XLA Ops:
  178.6 20.1 %collective-permute-start = (bf16[256,2304]{1,0:T(8,128)(2,1)}, bf16[256,2304]{1,0:T(8,128)(2,1)S(1)}, u32[]{:S(2)}, u32[]{:S(2)}) collective-permute-start(bf16[256,2304]{1,0:T(8,128)(2,1)} %get-tuple-element.17.last), channel_id=1, source_target_pairs={{0,1},{1,2},{2,3},{3,4},{4,5},{5,6},{6,7},{7,0},{8,15},{9,8},{10,9... | collective-permute-start | bytes 3538952 | tf_op jit(solution)/shard_map/ppermute | solution.py:338

commit v5 on v4

--- a/solution.py
+++ b/solution.py
@@ -27,7 +27,7 @@
 def kernel(
     n,
     x, dy, gate, up, w_gate, w_up, w_down,
-    dx, dw_gate, dw_up, dw_down, last,
+    dx, dw_gate, dw_up, dw_down, early, late,
     w_gu, w_d, d_gu, hid, dy_v, term, slots, stage,
     row_sem, wd_sem, wgu_sem, x_sem, out_sem, own_sem, rs_send, rs_recv, ag_send, ag_recv,
 ):
@@ -41,6 +41,7 @@
     peer = lax.rem(me + ahead + n, n)
     behind = lax.rem(me - ahead + n, n)
     hops = n - 2
+    turns = (hops - 1) * PIECES + 1
 
     def block_rows(step):
         return pl.ds(pl.multiple_of(lax.rem(me - ahead * step + 2 * n, n) * block, block), block)
@@ -88,11 +89,11 @@
     def columns(c):
         return pl.ds(pl.multiple_of(c * piece, piece), piece)
 
-    def ag_copy(hop, c, own=False, final=False):
+    def ag_copy(hop, c, own=False, into=None):
         place = dx.at[block_rows(hop + n - 1), columns(c)]
         return pltpu.make_async_remote_copy(
             src_ref=slots.at[n - 1, c] if own else place,
-            dst_ref=last.at[:, columns(c)] if final else place,
+            dst_ref=place if into is None else into,
             send_sem=ag_send.at[hop, c],
             recv_sem=ag_recv.at[hop, c],
             device_id={"tp": peer},
@@ -225,7 +226,6 @@
                 def _():
                     pltpu.make_async_copy(stage.at[slot], out.at[row, :], out_sem.at[slot]).start()
 
-    turns = hops * PIECES
     per_turn = -(-units // turns)
 
     def ag_step(turn, _):
@@ -237,17 +237,21 @@
         hop, c = lax.div(turn, PIECES), lax.rem(turn, PIECES)
         ag_copy(hop, c).wait_recv()
 
-        @pl.when(hop < hops - 2)
+        @pl.when(turn < turns - 2 - PIECES)
         def _():
             ag_copy(hop + 1, c).start()
 
-        @pl.when(hop == hops - 2)
-        def _():
-            ag_copy(hop + 1, c, final=True).start()
+        @pl.when(turn == turns - 2 - PIECES)
+        def _():
+            ag_copy(hop + 1, c, into=early).start()
+
+        @pl.when(turn == turns - 1 - PIECES)
+        def _():
+            ag_copy(hop + 1, c, into=late).start()
 
         return 0
 
-    assert FF_PIECES == PIECES + 1 and width == 2 * ff and tokens <= width
+    assert PIECES == 2 and FF_PIECES == 3 and n > 3 and width == 2 * ff and tokens <= width
     lax.fori_loop(0, turns, ag_step, 0)
 
     for unit in (units - 2, units - 1):
@@ -257,7 +261,7 @@
         for c in range(PIECES):
             rs_copy(hop, c).wait_send()
 
-            @pl.when(hop < hops)
+            @pl.when(hop * PIECES + c < turns)
             def _():
                 ag_copy(hop, c).wait_send()
 
@@ -268,23 +272,7 @@
         own_copy(c).wait()
 
 
-def outputs(n, dx_in, dw_gate_in, dw_up_in, dw_down_in, last, dx, dw_gate, dw_up, dw_down, wide, narrow, sems):
-    block = last.shape[0]
-    me = lax.axis_index("tp")
-    ahead = 1 - 2 * lax.rem(lax.axis_index("dp"), 2)
-    jobs = []
-    for i in range(n - 1):
-        rows = pl.ds(pl.multiple_of(lax.rem(me + ahead - ahead * i + n, n) * block, block), block)
-        jobs.append((dx_in.at[rows, :] if i < n - 2 else last, wide.at[pl.ds(i * block, block), :], dx.at[rows, :]))
-    spot = (n - 1) * block
-    for i in range(dw_down.shape[0] // TILE):
-        rows = pl.ds(i * TILE, TILE)
-        jobs.append((dw_down_in.at[rows, :], wide.at[pl.ds(spot + i * TILE, TILE), :], dw_down.at[rows, :]))
-    step = 2 * TILE
-    for j, (a, b) in enumerate(((dw_gate_in, dw_gate), (dw_up_in, dw_up))):
-        for i in range(b.shape[0] // step):
-            rows = pl.ds(i * step, step)
-            jobs.append((a.at[rows, :], narrow.at[j, rows, :], b.at[rows, :]))
+def move(jobs, sems):
     loads = [pltpu.make_async_copy(a, v, sems.at[0, k]) for k, (a, v, _) in enumerate(jobs)]
     stores = [pltpu.make_async_copy(v, b, sems.at[1, k]) for k, (_, v, b) in enumerate(jobs)]
     for load in loads:
@@ -296,6 +284,39 @@
         store.wait()
 
 
+def outputs(n, dx_in, dw_down_in, early, late, dx, dw_down, wide, sems):
+    block, piece = late.shape
+    me = lax.axis_index("tp")
+    ahead = 1 - 2 * lax.rem(lax.axis_index("dp"), 2)
+    left, right = pl.ds(0, piece), pl.ds(piece, piece)
+    jobs = []
+    for i in range(n - 1):
+        rows = pl.ds(pl.multiple_of(lax.rem(me + ahead - ahead * i + n, n) * block, block), block)
+        here = pl.ds(i * block, block)
+        if i < n - 3:
+            jobs.append((dx_in.at[rows, :], wide.at[here, :], dx.at[rows, :]))
+        else:
+            jobs.append((dx_in.at[rows, left] if i == n - 3 else late, wide.at[here, left], dx.at[rows, left]))
+        if i == n - 3:
+            jobs.append((early, wide.at[here, right], dx.at[rows, right]))
+    spot = (n - 1) * block
+    for i in range(dw_down.shape[0] // TILE):
+        rows = pl.ds(i * TILE, TILE)
+        jobs.append((dw_down_in.at[rows, :], wide.at[pl.ds(spot + i * TILE, TILE), :], dw_down.at[rows, :]))
+    move(jobs, sems)
+
+
+def more_outputs(dw_gate_in, dw_up_in, after, dw_gate, dw_up, narrow, sems):
+    del after
+    step = 2 * TILE
+    jobs = []
+    for j, (a, b) in enumerate(((dw_gate_in, dw_gate), (dw_up_in, dw_up))):
+        for i in range(b.shape[0] // step):
+            rows = pl.ds(i * step, step)
+            jobs.append((a.at[rows, :], narrow.at[j, rows, :], b.at[rows, :]))
+    move(jobs, sems)
+
+
 def solution(mesh):
     n, groups = mesh.shape["tp"], mesh.shape["dp"]
 
@@ -307,9 +328,9 @@
         results = [jax.ShapeDtypeStruct(a.shape, BF16) for a in (x, w_gate, w_up, w_down)]
         parts = pl.pallas_call(
             functools.partial(kernel, n),
-            out_shape=results + [jax.ShapeDtypeStruct((block, width), BF16)],
+            out_shape=results + [jax.ShapeDtypeStruct((block, piece), BF16)] * 2,
             in_specs=[hbm] * 7,
-            out_specs=[hbm] * 5,
+            out_specs=[hbm] * 6,
             scratch_shapes=[
                 pltpu.VMEM((width, 2 * ff), BF16),
                 pltpu.VMEM((ff, width), BF16),
@@ -335,23 +356,38 @@
             ),
         )(x, dy, gate, up, w_gate, w_up, w_down)
         ring = [(d * n + i, d * n + (i + 1 - 2 * (d % 2)) % n) for d in range(groups) for i in range(n)]
-        final = lax.ppermute(parts[4], ("dp", "tp"), ring)
-        dx, dw_gate, dw_up, dw_down = pl.pallas_call(
+        early, late = parts[4:]
+        right = lax.ppermute(early, ("dp", "tp"), ring)
+        last_left = lax.ppermute(late, ("dp", "tp"), ring)
+        last_right = lax.ppermute(right, ("dp", "tp"), ring)
+        cost = pl.CostEstimate(flops=2**33, bytes_accessed=2**24, transcendentals=0)
+        dx, dw_down = pl.pallas_call(
             functools.partial(outputs, n),
-            out_shape=results,
-            in_specs=[hbm] * 5,
-            out_specs=[hbm] * 4,
+            out_shape=[results[0], results[3]],
+            in_specs=[hbm] * 4,
+            out_specs=[hbm] * 2,
             scratch_shapes=[
                 pltpu.VMEM(((n - 1) * block + ff, width), BF16),
-                pltpu.VMEM((2, width, ff), BF16),
-                pltpu.SemaphoreType.DMA((2, n - 1 + ff // TILE + width // TILE)),
+                pltpu.SemaphoreType.DMA((2, n + ff // TILE)),
             ],
-            cost_estimate=pl.CostEstimate(flops=2**34, bytes_accessed=2**25, transcendentals=0),
+            cost_estimate=cost,
             compiler_params=pltpu.CompilerParams(has_side_effects=True),
-        )(*parts)
+        )(parts[0], parts[3], early, late)
+        dw_gate, dw_up = pl.pallas_call(
+            more_outputs,
+            out_shape=results[1:3],
+            in_specs=[hbm] * 3,
+            out_specs=[hbm] * 2,
+            scratch_shapes=[pltpu.VMEM((2, width, ff), BF16), pltpu.SemaphoreType.DMA((2, width // TILE))],
+            cost_estimate=cost,
+            compiler_params=pltpu.CompilerParams(has_side_effects=True),
+        )(parts[1], parts[2], dw_down)
         me = lax.axis_index("tp")
         ahead = 1 - 2 * lax.rem(lax.axis_index("dp"), 2)
-        dx = lax.dynamic_update_slice(dx, final, (lax.rem(me + 2 * ahead + n, n) * block, 0))
+        end = lax.rem(me + 2 * ahead + n, n) * block
+        dx = lax.dynamic_update_slice(dx, right, (lax.rem(me + 3 * ahead + n, n) * block, piece))
+        dx = lax.dynamic_update_slice(dx, last_left, (end, 0))
+        dx = lax.dynamic_update_slice(dx, last_right, (end, piece))
         return dx, dw_gate, dw_up, dw_down
 
     tokens, columns, rows = P("dp", None), P(None, "tp"), P("tp", None)

time: 200 us -> 199 us (level)
  Pallas kernels: 195 us -> 189 us
    pallas_call x1, Pallas kernels: 178 us -> 172 us  [step(): pl.pallas_call(functools.partial(kernel, n), out_shape=results + [jax.Sha...]
    ppermute x1 -> x3, starting transfers between devices: 3.29 us -> 4.87 us  [the longest x1 3.29 us: step(): right = lax.ppermute(early, ('dp', 'tp'), ring)]
    pallas_call x1 -> x2, Pallas kernels: 16.8 us -> 17.4 us  [the longest x1 9.09 us: step(): pl.pallas_call(functools.partial(outputs, n), out_shape=[results[0], resu...]
  transfers between devices with their start and end apart: 1 -> 3, of which waited for: 0 -> 0; matrix products, arithmetic and copies ran while one was open for 0% -> 1% of each run, Pallas kernels for 8% -> 9%
where the time goes in v5:
time: 199 us; the launch traced here: 197 us
  Pallas kernels  189 us (95%)
  starting transfers between devices  4.87 us (2%)
  local copies, waits for them, and re-layouts  2.59 us (1%)
    pallas_call x1, Pallas kernels, step(): pl.pallas_call(functools.partial(kernel, n), out_shape=results + [jax.Sha...  172 us
    pallas_call x1, Pallas kernels, step(): pl.pallas_call(functools.partial(outputs, n), out_shape=[results[0], resu...  9.09 us
    pallas_call x1, Pallas kernels, step(): pl.pallas_call(more_outputs, out_shape=results[1:3], in_specs=[hbm] * 3,...  8.3 us
  transfers between devices with their start and end apart: 3, of which 0 were waited for; matrix products, arithmetic and copies ran while one was open for 1% of the time, Pallas kernels for 9%

profile of v5, /device:TPU:21, one launch (start us, length us, event | category | flops | bytes accessed | tf_op | source)
XLA Modules:
  0.0 197.1 jit_solution(10818101767938626882)
XLA Ops:
  0.6 171.6 %shard_map.102 = (bf16[2048,2304]{1,0:T(8,128)(2,1)}, bf16[2304,1152]{1,0:T(8,128)(2,1)}, bf16[2304,1152]{1,0:T(8,128)(2,1)}, bf16[1152,2304]{1,0:T(8,128)(2,1)}...) custom-call(bf16[2048,2304]{1,0:T(8,128)(2,1)} %x.1, bf16[2048,2304]{1,0:T(8,128)(2,1)} %dy.1, ...), custom_call_target="tpu_custom_call" | custom-call | tf_op jit(solution)/shard_map/pallas_call | solution.py:329
  172.2 3.3 %collective-permute-start = (bf16[256,1152]{1,0:T(8,128)(2,1)}, bf16[256,1152]{1,0:T(8,128)(2,1)S(1)}, u32[]{:S(2)}, u32[]{:S(2)}) collective-permute-start(bf16[256,1152]{1,0:T(8,128)(2,1)} %get-tuple-element.16.early), channel_id=1, source_target_pairs={{0,1},{1,2},{2,3},{3,4},{4,5},{5,6},{6,7},{7,0},{8,15},{9,8},{10,9... | collective-permute-start | bytes 1769480 | tf_op jit(solution)/shard_map/ppermute | solution.py:360
  175.5 1.0 collective-permute-start.1
  176.5 9.1 %shard_map.103 = (bf16[2048,2304]{1,0:T(8,128)(2,1)}, bf16[1152,2304]{1,0:T(8,128)(2,1)}) custom-call(bf16[2048,2304]{1,0:T(8,128)(2,1)} %get-tuple-element.14.dx_in, bf16[1152,2304]{1,0:T(8,128)(2,1)} %get-tuple-element.15.dw_down_in, bf16[256,1152]{1,0:T(8,128)(2,1)} %get-tuple-element.16.early, bf16[256,1152]{1,0:T(8,128)(2,1)} %get-tuple-element.17.late), custom_call_target="tpu_custom_call" | custom-call | flops 8589934592 | bytes 16777216 | tf_op jit(solution)/shard_map/pallas_call | solution.py:364
  185.6 0.0 collective-permute-done
  185.6 0.6 collective-permute-start.2
  186.2 8.3 %shard_map.104 = (bf16[2304,1152]{1,0:T(8,128)(2,1)}, bf16[2304,1152]{1,0:T(8,128)(2,1)}) custom-call(bf16[2304,1152]{1,0:T(8,128)(2,1)} %get-tuple-element.19.dw_gate_in, bf16[2304,1152]{1,0:T(8,128)(2,1)} %get-tuple-element.20.dw_up_in, bf16[1152,2304]{1,0:T(8,128)(2,1)} %get-tuple-element.13.after), custom_call_target="tpu_custom_call" | custom-call | flops 8589934592 | bytes 16777216 | tf_op jit(solution)/shard_map/pallas_call | solution.py:376
  194.6 0.9 constant_dynamic-update-slice_fusion.1
  195.4 0.0 collective-permute-done.1
  195.4 0.9 constant_dynamic-update-slice_fusion.2
  196.3 0.0 collective-permute-done.2
  196.3 0.9 constant_dynamic-update-slice_fusion
Async XLA Ops:
  172.2 13.3 %collective-permute-start = (bf16[256,1152]{1,0:T(8,128)(2,1)}, bf16[256,1152]{1,0:T(8,128)(2,1)S(1)}, u32[]{:S(2)}, u32[]{:S(2)}) collective-permute-start(bf16[256,1152]{1,0:T(8,128)(2,1)} %get-tuple-element.16.early), channel_id=1, source_target_pairs={{0,1},{1,2},{2,3},{3,4},{4,5},{5,6},{6,7},{7,0},{8,15},{9,8},{10,9... | collective-permute-start | bytes 1769480 | tf_op jit(solution)/shard_map/ppermute | solution.py:360
  175.5 19.9 %collective-permute-start.1 = (bf16[256,1152]{1,0:T(8,128)(2,1)}, bf16[256,1152]{1,0:T(8,128)(2,1)S(1)}, u32[]{:S(2)}, u32[]{:S(2)}) collective-permute-start(bf16[256,1152]{1,0:T(8,128)(2,1)} %get-tuple-element.17.late), channel_id=1, source_target_pairs={{0,1},{1,2},{2,3},{3,4},{4,5},{5,6},{6,7},{7,0},{8,15},{9,8},{10,9... | collective-permute-start | bytes 1769480 | tf_op jit(solution)/shard_map/ppermute | solution.py:361
  185.6 10.7 %collective-permute-start.2 = (bf16[256,1152]{1,0:T(8,128)(2,1)S(1)}, bf16[256,1152]{1,0:T(8,128)(2,1)S(1)}, u32[]{:S(2)}, u32[]{:S(2)}) collective-permute-start(bf16[256,1152]{1,0:T(8,128)(2,1)S(1)} %collective-permute-done), channel_id=1, source_target_pairs={{0,1},{1,2},{2,3},{3,4},{4,5},{5,6},{6,7},{7,0},{8,15},{9,8},{10,9... | collective-permute-start | bytes 1769480 | tf_op jit(solution)/shard_map/ppermute | solution.py:362

commit v6 on v5

--- a/solution.py
+++ b/solution.py
@@ -29,7 +29,7 @@
     x, dy, gate, up, w_gate, w_up, w_down,
     dx, dw_gate, dw_up, dw_down, early, late,
     w_gu, w_d, d_gu, hid, dy_v, term, slots, stage,
-    row_sem, wd_sem, wgu_sem, x_sem, out_sem, own_sem, rs_send, rs_recv, ag_send, ag_recv,
+    row_sem, wd_sem, wgu_sem, x_sem, out_sem, dx_sem, rs_send, rs_recv, ag_send, ag_recv,
 ):
     tokens, width = dy_v.shape
     ff = w_d.shape[0]
@@ -89,19 +89,19 @@
     def columns(c):
         return pl.ds(pl.multiple_of(c * piece, piece), piece)
 
-    def ag_copy(hop, c, own=False, into=None):
-        place = dx.at[block_rows(hop + n - 1), columns(c)]
+    def ag_copy(hop, c, into=None):
         return pltpu.make_async_remote_copy(
-            src_ref=slots.at[n - 1, c] if own else place,
-            dst_ref=place if into is None else into,
+            src_ref=slots.at[lax.rem(hop + n - 1, n + 1), c],
+            dst_ref=slots.at[lax.rem(hop + n, n + 1), c] if into is None else into,
             send_sem=ag_send.at[hop, c],
             recv_sem=ag_recv.at[hop, c],
             device_id={"tp": peer},
             device_id_type=MESH,
         )
 
-    def own_copy(c):
-        return pltpu.make_async_copy(slots.at[n - 1, c], dx.at[block_rows(n - 1), columns(c)], own_sem.at[c])
+    def dx_copy(step, c):
+        slot = lax.rem(step, n + 1)
+        return pltpu.make_async_copy(slots.at[slot, c], dx.at[block_rows(step), columns(c)], dx_sem.at[slot, c])
 
     barrier = pltpu.get_barrier_semaphore()
     for other in (peer, behind):
@@ -171,6 +171,7 @@
         def _():
             for c in range(PIECES):
                 rs_copy(step - 1, c).wait_recv()
+                rs_copy(step - 1, c).wait_send()
                 total = slots[step, c].astype(F32) + term[:, c * piece : (c + 1) * piece]
                 slots[step, c] = total.astype(BF16)
 
@@ -180,8 +181,8 @@
 
                 @pl.when(step == n - 1)
                 def _():
-                    ag_copy(0, c, own=True).start()
-                    own_copy(c).start()
+                    ag_copy(0, c).start()
+                    dx_copy(n - 1, c).start()
 
         return 0
 
@@ -237,6 +238,10 @@
         hop, c = lax.div(turn, PIECES), lax.rem(turn, PIECES)
         ag_copy(hop, c).wait_recv()
 
+        @pl.when(turn < turns - 2)
+        def _():
+            dx_copy(hop + n, c).start()
+
         @pl.when(turn < turns - 2 - PIECES)
         def _():
             ag_copy(hop + 1, c).start()
@@ -259,17 +264,19 @@
 
     def sends(hop, _):
         for c in range(PIECES):
-            rs_copy(hop, c).wait_send()
-
             @pl.when(hop * PIECES + c < turns)
             def _():
                 ag_copy(hop, c).wait_send()
+
+            @pl.when(hop * PIECES + c < turns - 2)
+            def _():
+                dx_copy(hop + n, c).wait()
 
         return 0
 
     lax.fori_loop(0, n - 1, sends, 0)
     for c in range(PIECES):
-        own_copy(c).wait()
+        dx_copy(n - 1, c).wait()
 
 
 def move(jobs, sems):
@@ -338,14 +345,14 @@
                 pltpu.VMEM((tokens, ff), BF16),
                 pltpu.VMEM((tokens, width), BF16),
                 pltpu.VMEM((block, width), F32),
-                pltpu.VMEM((n, PIECES, block, piece), BF16),
+                pltpu.VMEM((n + 1, PIECES, block, piece), BF16),
                 pltpu.VMEM((2, TILE, ff), BF16),
                 pltpu.SemaphoreType.DMA((2, 3)),
                 pltpu.SemaphoreType.DMA((FF_PIECES,)),
                 pltpu.SemaphoreType.DMA((PIECES + 1, 2)),
                 pltpu.SemaphoreType.DMA((n,)),
                 pltpu.SemaphoreType.DMA((2,)),
-                pltpu.SemaphoreType.DMA((PIECES,)),
+                pltpu.SemaphoreType.DMA((n + 1, PIECES)),
                 pltpu.SemaphoreType.DMA((n, PIECES)),
                 pltpu.SemaphoreType.DMA((n, PIECES)),
                 pltpu.SemaphoreType.DMA((n, PIECES)),

time: 199 us -> 200 us (level)
  no operation moved by 1% of the time
where the time goes in v6:
time: 200 us; the launch traced here: 197 us
  Pallas kernels  189 us (94%)
  starting transfers between devices  4.92 us (2%)
  local copies, waits for them, and re-layouts  2.59 us (1%)
    pallas_call x1, Pallas kernels, step(): pl.pallas_call(functools.partial(kernel, n), out_shape=results + [jax.Sha...  172 us
    pallas_call x1, Pallas kernels, step(): pl.pallas_call(functools.partial(outputs, n), out_shape=[results[0], resu...  9.09 us
    pallas_call x1, Pallas kernels, step(): pl.pallas_call(more_outputs, out_shape=results[1:3], in_specs=[hbm] * 3,...  8.3 us
  transfers between devices with their start and end apart: 3, of which 0 were waited for; matrix products, arithmetic and copies ran while one was open for 1% of the time, Pallas kernels for 9%

profile of v6, /device:TPU:21, one launch (start us, length us, event | category | flops | bytes accessed | tf_op | source)
XLA Modules:
  0.0 197.3 jit_solution(8787056097459670991)
XLA Ops:
  0.6 171.7 %shard_map.102 = (bf16[2048,2304]{1,0:T(8,128)(2,1)}, bf16[2304,1152]{1,0:T(8,128)(2,1)}, bf16[2304,1152]{1,0:T(8,128)(2,1)}, bf16[1152,2304]{1,0:T(8,128)(2,1)}...) custom-call(bf16[2048,2304]{1,0:T(8,128)(2,1)} %x.1, bf16[2048,2304]{1,0:T(8,128)(2,1)} %dy.1, ...), custom_call_target="tpu_custom_call" | custom-call | tf_op jit(solution)/shard_map/pallas_call | solution.py:336
  172.4 3.3 %collective-permute-start = (bf16[256,1152]{1,0:T(8,128)(2,1)}, bf16[256,1152]{1,0:T(8,128)(2,1)S(1)}, u32[]{:S(2)}, u32[]{:S(2)}) collective-permute-start(bf16[256,1152]{1,0:T(8,128)(2,1)} %get-tuple-element.16.early), channel_id=1, source_target_pairs={{0,1},{1,2},{2,3},{3,4},{4,5},{5,6},{6,7},{7,0},{8,15},{9,8},{10,9... | collective-permute-start | bytes 1769480 | tf_op jit(solution)/shard_map/ppermute | solution.py:367
  175.7 1.0 collective-permute-start.1
  176.7 9.1 %shard_map.103 = (bf16[2048,2304]{1,0:T(8,128)(2,1)}, bf16[1152,2304]{1,0:T(8,128)(2,1)}) custom-call(bf16[2048,2304]{1,0:T(8,128)(2,1)} %get-tuple-element.14.dx_in, bf16[1152,2304]{1,0:T(8,128)(2,1)} %get-tuple-element.15.dw_down_in, bf16[256,1152]{1,0:T(8,128)(2,1)} %get-tuple-element.16.early, bf16[256,1152]{1,0:T(8,128)(2,1)} %get-tuple-element.17.late), custom_call_target="tpu_custom_call" | custom-call | flops 8589934592 | bytes 16777216 | tf_op jit(solution)/shard_map/pallas_call | solution.py:371
  185.8 0.0 collective-permute-done
  185.8 0.6 collective-permute-start.2
  186.4 8.3 %shard_map.104 = (bf16[2304,1152]{1,0:T(8,128)(2,1)}, bf16[2304,1152]{1,0:T(8,128)(2,1)}) custom-call(bf16[2304,1152]{1,0:T(8,128)(2,1)} %get-tuple-element.19.dw_gate_in, bf16[2304,1152]{1,0:T(8,128)(2,1)} %get-tuple-element.20.dw_up_in, bf16[1152,2304]{1,0:T(8,128)(2,1)} %get-tuple-element.13.after), custom_call_target="tpu_custom_call" | custom-call | flops 8589934592 | bytes 16777216 | tf_op jit(solution)/shard_map/pallas_call | solution.py:383
  194.7 0.9 constant_dynamic-update-slice_fusion.1
  195.6 0.0 collective-permute-done.1
  195.6 0.9 constant_dynamic-update-slice_fusion.2
  196.5 0.0 collective-permute-done.2
  196.5 0.9 constant_dynamic-update-slice_fusion
Async XLA Ops:
  172.4 13.4 %collective-permute-start = (bf16[256,1152]{1,0:T(8,128)(2,1)}, bf16[256,1152]{1,0:T(8,128)(2,1)S(1)}, u32[]{:S(2)}, u32[]{:S(2)}) collective-permute-start(bf16[256,1152]{1,0:T(8,128)(2,1)} %get-tuple-element.16.early), channel_id=1, source_target_pairs={{0,1},{1,2},{2,3},{3,4},{4,5},{5,6},{6,7},{7,0},{8,15},{9,8},{10,9... | collective-permute-start | bytes 1769480 | tf_op jit(solution)/shard_map/ppermute | solution.py:367
  175.7 19.9 %collective-permute-start.1 = (bf16[256,1152]{1,0:T(8,128)(2,1)}, bf16[256,1152]{1,0:T(8,128)(2,1)S(1)}, u32[]{:S(2)}, u32[]{:S(2)}) collective-permute-start(bf16[256,1152]{1,0:T(8,128)(2,1)} %get-tuple-element.17.late), channel_id=1, source_target_pairs={{0,1},{1,2},{2,3},{3,4},{4,5},{5,6},{6,7},{7,0},{8,15},{9,8},{10,9... | collective-permute-start | bytes 1769480 | tf_op jit(solution)/shard_map/ppermute | solution.py:368
  185.8 10.7 %collective-permute-start.2 = (bf16[256,1152]{1,0:T(8,128)(2,1)S(1)}, bf16[256,1152]{1,0:T(8,128)(2,1)S(1)}, u32[]{:S(2)}, u32[]{:S(2)}) collective-permute-start(bf16[256,1152]{1,0:T(8,128)(2,1)S(1)} %collective-permute-done), channel_id=1, source_target_pairs={{0,1},{1,2},{2,3},{3,4},{4,5},{5,6},{6,7},{7,0},{8,15},{9,8},{10,9... | collective-permute-start | bytes 1769480 | tf_op jit(solution)/shard_map/ppermute | solution.py:369
